TPU v7x, 32 devices: a whole 2x2x4 slice. The times are simulated.
32 devices in a mesh: aa: 8 (over z, x), ba: 4 (over y, core).
Axes of the slice: x: 2, y: 2, z: 4, core: 2. Of those that a mesh axis runs over, the one named last changes fastest.
Arguments:
- residual_a: bfloat16 [64, 4096], P('ba', 'aa'), may hold values from -160 to 160
- residual_b: bfloat16 [64, 3584], P(('aa', 'ba')), may hold values from -160 to 160
- encoder_a: bfloat16 [4096, 16384], P('ba', 'aa'), may hold values from -1 to 1
- bias_a: float32 [16384], P('aa'), may hold values from -12 to 12
- encoder_b: bfloat16 [3584, 16384], P('aa', 'ba'), may hold values from -1 to 1
- bias_b: float32 [16384], P('ba'), may hold values from -12 to 12
Outputs:
- match_score: float32 [16384, 16384], P('aa', 'ba')
- row_level: float32 [16384], P('aa')
- column_level: float32 [16384], P('ba')
All inputs are finite; a program needn't handle non-finite values.
Results may differ from a plain program's by a relative error of at most 0.0004.
The roundings to bfloat16 on the way count: a program that leaves them out, or rounds other values in their place, can miss the bound.
Values may be sent and summed in bfloat16 or wider, within the bound.
No kernel may reach another device: no remote copies, remote signals or barrier semaphores. Data moves between devices by JAX's collectives and lax.ppermute only.
A program may use at most 128 MiB of HBM per device.

v0:
```python
import jax
import jax.numpy as jnp
from jax import lax
from jax.sharding import PartitionSpec as P

INV_TEMP = 256


epsilon = 1e-05


def per_device(residual_a, residual_b, encoder_a, bias_a, encoder_b, bias_b):
    rows_a = lax.all_gather(residual_a, "aa", axis=1, tiled=True)
    inputs = rows_a
    encoded_a = jnp.dot(
        inputs,
        lax.all_gather(encoder_a, "ba", axis=0, tiled=True),
        preferred_element_type=jnp.float32,
    )
    fired_a = jnp.maximum(encoded_a + bias_a[None, :], 0.0)
    rows_b = lax.all_gather(residual_b, "ba", axis=0, tiled=True)
    columns_b = lax.all_to_all(rows_b, "aa", split_axis=1, concat_axis=0, tiled=True)
    inputs = columns_b
    encoded_b = lax.psum_scatter(
        jnp.dot(inputs, encoder_b, preferred_element_type=jnp.float32),
        "aa",
        scatter_dimension=0,
        tiled=True,
    )
    fired_b = jnp.maximum(encoded_b + bias_b[None, :], 0.0)
    token_total = float(rows_a.shape[0] * lax.axis_size("ba"))
    mean_a = lax.psum(jnp.sum(fired_a, 0), "ba") / token_total
    mean_b = lax.psum(jnp.sum(fired_b, 0), "aa") / token_total
    centered_a = fired_a - mean_a[None, :]
    centered_b = fired_b - mean_b[None, :]
    spread_a = lax.psum(jnp.sum(centered_a * centered_a, 0), "ba") / token_total
    spread_b = lax.psum(jnp.sum(centered_b * centered_b, 0), "aa") / token_total
    unit_a = (centered_a * lax.rsqrt(spread_a + epsilon)[None, :]).astype(jnp.bfloat16)
    unit_b = (centered_b * lax.rsqrt(spread_b + epsilon)[None, :]).astype(jnp.bfloat16)
    every_a = lax.all_gather(unit_a, "ba", axis=0, tiled=True)
    correlation = (
        lax.dot_general(
            every_a,
            lax.all_gather(unit_b, "aa", axis=0, tiled=True),
            (((0,), (0,)), ((), ())),
            preferred_element_type=jnp.float32,
        )
        / token_total
    )
    scores = correlation * INV_TEMP
    row_local = jnp.max(scores, axis=1)
    column_local = jnp.max(scores, axis=0)
    row_top = lax.pmax(row_local, "ba")
    column_top = lax.pmax(column_local, "aa")
    row_mass = lax.psum(jnp.sum(jnp.exp(scores - row_top[:, None]), axis=1), "ba")
    column_mass = lax.psum(jnp.sum(jnp.exp(scores - column_top[None, :]), axis=0), "aa")
    row_level = (row_top + jnp.log(row_mass)) / INV_TEMP
    column_level = (column_top + jnp.log(column_mass)) / INV_TEMP
    match_score = correlation - 0.5 * (row_level[:, None] + column_level[None, :])
    return (match_score, row_level, column_level)


def solution(mesh):
    return jax.shard_map(
        per_device,
        mesh=mesh,
        in_specs=(
            P("ba", "aa"),
            P(("aa", "ba"), None),
            P("ba", "aa"),
            P("aa"),
            P("aa", "ba"),
            P("ba"),
        ),
        out_specs=(P("aa", "ba"), P("aa"), P("ba")),
        check_vma=False,
    )
```

profile of v0, /device:TPU:0, one launch (start us, length us, event | category | flops | bytes accessed | tf_op | source)
XLA Modules:
  0.0 375.0 jit_solution(1914857120567517789)
XLA Ops:
  8.0 6.5 %all-gather = bf16[4,2,3584]{2,1,0:T(2,128)(2,1)S(1)} all-gather(bf16[1,2,3584]{2,1,0:T(2,128)(2,1)} %bitcast.11), channel_id=1, replica_groups=mesh['aa'=8,'ba'=4] {'ba'}, dimensions={0}, use_global_device_ids=true | all-gather | bytes 71680 | tf_op jit(solution)/shard_map/all_gather | solution.py:21
  14.7 12.9 %all_to_all.19 = bf16[8,8,448]{2,0,1:T(8,128)(2,1)S(1)} all-to-all(bf16[8,8,448]{2,0,1:T(8,128)(2,1)S(1)} %copy.10), channel_id=1, replica_groups=mesh['aa'=8,'ba'=4] {'aa'}, dimensions={1} | all-to-all | bytes 114688 | tf_op jit(solution)/shard_map/all_to_all | solution.py:22
  27.6 3.8 %fusion.2 = f32[64,4096]{1,0:T(8,128)} fusion(bf16[448,4096]{1,0:T(8,128)(2,1)} %param.10, bf16[8,8,448]{2,0,1:T(8,128)(2,1)S(1)} %all_to_all.19), kind=kOutput, calls=%fused_computation.13 | convolution fusion | flops 234881024 | bytes 4775936 | tf_op jit(solution)/shard_map/dot_general | solution.py:25
  31.5 0.5 all-gather.3.cloned.1.call-update
  32.0 30.8 %all_gather.15 = bf16[16,4096]{1,0:T(8,128)(2,1)S(1)} all-gather(bf16[16,512]{1,0:T(8,128)(2,1)} %param.6), channel_id=1, replica_groups=mesh['aa'=8,'ba'=4] {'aa'}, dimensions={1}, use_global_device_ids=true | all-gather | bytes 147456 | tf_op jit(solution)/shard_map/all_gather | solution.py:13
  62.8 30.5 %reduce-scatter.2.cloned.1.call-done = f32[8,4096]{1,0:T(8,128)} async-done(((f32[64,4096]{1,0:T(8,128)}), f32[8,4096]{1,0:T(8,128)}) %reduce-scatter.2.cloned.1.call-update) | async-done | bytes 131088 | tf_op jit(solution)/shard_map/reduce_scatter | solution.py:24
  93.3 1.0 fusion.1
  94.3 35.0 %psum.44 = f32[4096]{0:T(1024)S(1)} all-reduce(f32[4096]{0:T(1024)S(1)} %fusion.1), channel_id=1, replica_groups=mesh['aa'=8,'ba'=4] {'aa'}, use_global_device_ids=true, to_apply=%region_6.0 | all-reduce | flops 4096 | bytes 32768 | tf_op jit(solution)/shard_map/psum | solution.py:33
  129.3 1.0 multiply_reduce_fusion.2
  130.3 33.0 %psum.45 = f32[4096]{0:T(1024)S(1)} all-reduce(f32[4096]{0:T(1024)S(1)} %multiply_reduce_fusion.2), channel_id=1, replica_groups=mesh['aa'=8,'ba'=4] {'aa'}, use_global_device_ids=true, to_apply=%region_8.0 | all-reduce | flops 4096 | bytes 32768 | tf_op jit(solution)/shard_map/psum | solution.py:37
  163.3 0.9 multiply_convert_fusion
  164.2 31.3 %all_gather.19 = bf16[64,4096]{1,0:T(8,128)(2,1)S(1)} all-gather(bf16[8,4096]{1,0:T(8,128)(2,1)S(1)} %multiply_convert_fusion), channel_id=1, replica_groups=mesh['aa'=8,'ba'=4] {'aa'}, dimensions={0}, use_global_device_ids=true | all-gather | bytes 589824 | tf_op jit(solution)/shard_map/all_gather | solution.py:44
  195.5 8.1 %fusion.4 = (f32[2048]{0:T(1024)S(1)}, f32[16,2048]{1,0:T(8,128)S(1)}) fusion(f32[2048]{0:T(1024)} %param.9, bf16[16,4096]{1,0:T(8,128)(2,1)S(1)} %all_gather.15, bf16[4096,2048]{1,0:T(8,128)(2,1)} %all-gather.3.cloned.1.call-done), kind=kOutput, calls=%fused_computation.21 | convolution fusion | flops 268531712 | bytes 17055744 | tf_op jit(solution)/shard_map/dot_general | solution.py:15
  203.6 5.8 %psum.42 = f32[2048]{0:T(1024)S(1)} all-reduce(f32[2048]{0:T(1024)S(1)} %get-tuple-element.5), channel_id=1, replica_groups=mesh['aa'=8,'ba'=4] {'ba'}, use_global_device_ids=true, to_apply=%region_1.0 | all-reduce | flops 2048 | bytes 16384 | tf_op jit(solution)/shard_map/psum | solution.py:32
  209.4 6.7 %psum.43 = f32[2048]{0:T(1024)S(1)} all-reduce(f32[2048]{0:T(1024)S(1)} %multiply_reduce_fusion.3), channel_id=1, replica_groups=mesh['aa'=8,'ba'=4] {'ba'}, use_global_device_ids=true, to_apply=%region_3.0 | all-reduce | flops 2048 | bytes 16384 | tf_op jit(solution)/shard_map/psum | solution.py:36
  216.1 5.8 %all_gather.17 = bf16[64,2048]{1,0:T(8,128)(2,1)S(1)} all-gather(bf16[16,2048]{1,0:T(8,128)(2,1)S(1)} %multiply_convert_fusion.1), channel_id=1, replica_groups=mesh['aa'=8,'ba'=4] {'ba'}, dimensions={0}, use_global_device_ids=true | all-gather | bytes 327680 | tf_op jit(solution)/shard_map/all_gather | solution.py:40
  221.9 14.1 %multiply_reduce_fusion.1 = (f32[2048]{0:T(1024)S(1)}, f32[2048,4096]{1,0:T(8,128)}) fusion(bf16[64,2048]{1,0:T(8,128)(2,1)S(1)} %all_gather.17, bf16[64,4096]{1,0:T(8,128)(2,1)S(1)} %all_gather.19), kind=kOutput, calls=%fused_computation.4 | convolution fusion | flops 1090516992 | bytes 34349056 | tf_op jit(solution)/shard_map/dot_general | solution.py:42
  235.9 6.7 %pmax.14 = f32[2048]{0:T(1024)S(1)} all-reduce(f32[2048]{0:T(1024)S(1)} %get-tuple-element.7), channel_id=1, replica_groups=mesh['aa'=8,'ba'=4] {'ba'}, use_global_device_ids=true, to_apply=%region_10.0 | all-reduce | flops 2048 | bytes 16384 | tf_op jit(solution)/shard_map/pmax | solution.py:53
  242.6 15.1 %exponential_reduce_fusion.1 = (f32[2048]{0:T(1024)S(1)}, f32[4096]{0:T(1024)S(1)}) fusion(f32[2048,4096]{1,0:T(8,128)} %get-tuple-element.8, f32[2048]{0:T(1024)S(1)} %pmax.14), kind=kLoop, calls=%fused_computation.2 | loop fusion | flops 33548288 | bytes 33587200 | tf_op jit(solution)/shard_map/reduce_sum | solution.py:55
  257.8 5.8 %psum.46 = f32[2048]{0:T(1024)S(1)} all-reduce(f32[2048]{0:T(1024)S(1)} %get-tuple-element.3), channel_id=1, replica_groups=mesh['aa'=8,'ba'=4] {'ba'}, use_global_device_ids=true, to_apply=%region_12.0 | all-reduce | flops 2048 | bytes 16384 | tf_op jit(solution)/shard_map/psum | solution.py:55
  263.6 33.0 %pmax.15 = f32[4096]{0:T(1024)S(1)} all-reduce(f32[4096]{0:T(1024)S(1)} %get-tuple-element.4), channel_id=1, replica_groups=mesh['aa'=8,'ba'=4] {'aa'}, use_global_device_ids=true, to_apply=%region_14.0 | all-reduce | flops 4096 | bytes 32768 | tf_op jit(solution)/shard_map/pmax | solution.py:54
  296.5 13.7 %exponential_reduce_fusion = f32[4096]{0:T(1024)S(1)} fusion(f32[2048,4096]{1,0:T(8,128)} %get-tuple-element.8, f32[4096]{0:T(1024)S(1)} %pmax.15), kind=kLoop, calls=%fused_computation.1 | loop fusion | flops 25161728 | bytes 33587200 | tf_op jit(solution)/shard_map/reduce_sum | solution.py:56
  310.3 33.0 %psum.47 = f32[4096]{0:T(1024)S(1)} all-reduce(f32[4096]{0:T(1024)S(1)} %exponential_reduce_fusion), channel_id=1, replica_groups=mesh['aa'=8,'ba'=4] {'aa'}, use_global_device_ids=true, to_apply=%region_16.0 | all-reduce | flops 4096 | bytes 32768 | tf_op jit(solution)/shard_map/psum | solution.py:56
  343.3 24.3 %multiply_subtract_fusion = f32[2048,4096]{1,0:T(8,128)} fusion(f32[2048,4096]{1,0:T(8,128)} %get-tuple-element.8, f32[4096]{0:T(1024)S(1)} %add_multiply_fusion, f32[2048]{0:T(1024)S(1)} %add_multiply_fusion.1), kind=kLoop, calls=%fused_computation | loop fusion | flops 33554432 | bytes 67133440 | tf_op jit(solution)/shard_map/sub | solution.py:59
  (18 shorter events, 0.4 us)
Async XLA Ops:
  8.0 85.3 %reduce-scatter.2.cloned.1.call-start = ((), (), s32[]{:S(2)}) async-start(), calls=%async_computation.3 | async-start | bytes 1179648 | tf_op jit(solution)/shard_map/reduce_scatter | solution.py:24
  31.4 164.1 %all-gather.3.cloned.1.call-start = ((), (), s32[]{:S(2)}) async-start(), calls=%async_computation.2 | async-start | bytes 20971520 | tf_op jit(solution)/shard_map/all_gather | solution.py:17
  263.5 104.0 %copy-start.1 = (f32[2048]{0:T(1024)}, f32[2048]{0:T(1024)S(1)}, u32[]{:S(2)}) copy-start(f32[2048]{0:T(1024)S(1)} %add_multiply_fusion.1) | copy-start | bytes 24580
  343.3 24.3 %copy-start = (f32[4096]{0:T(1024)}, f32[4096]{0:T(1024)S(1)}, u32[]{:S(2)}) copy-start(f32[4096]{0:T(1024)S(1)} %add_multiply_fusion) | copy-start | bytes 49156
Sparse Core Ops, SparseCore 0:
  31.5 61.7 reduce-scatter.1
Sparse Core Ops, SparseCore 1:
  33.5 103.3 all-gather.2
where the time goes:
time: 376 us; the launch traced here: 375 us
  blocking collectives  246 us (65%)
  other arithmetic  56.1 us (15%)
  waiting for transfers between devices  31.1 us (8%)
  matrix products  25.9 us (7%)
  between operations  15.6 us (4%)
    psum x1, blocking collectives, per_device(): mean_b = lax.psum(jnp.sum(fired_b, 0), 'aa') / token_total  35 us
    psum x1, blocking collectives, per_device(): spread_b = lax.psum(jnp.sum(centered_b * centered_b, 0), 'aa') / token_total  33 us
    pmax x1, blocking collectives, per_device(): column_top = lax.pmax(column_local, 'aa')  33 us
    psum x1, blocking collectives, per_device(): lax.psum(jnp.sum(jnp.exp(scores - column_top[None, :]), axis=0), 'aa')  33 us
    all_gather x1, blocking collectives, per_device(): lax.all_gather(unit_b, 'aa', axis=0, tiled=True)  31.3 us
    all_gather x1, blocking collectives, per_device(): rows_a = lax.all_gather(residual_a, 'aa', axis=1, tiled=True)  30.8 us
    reduce_scatter x1, waiting for transfers between devices, per_device(): lax.psum_scatter(jnp.dot(inputs, encoder_b, preferred_element_type=jnp.fl...  30.5 us
    sub x1, other arithmetic, per_device(): correlation - 0.5 * (row_level[:, None] + column_level[None, :])  24.3 us
  transfers between devices with their start and end apart: 2, of which 1 were waited for; matrix products, arithmetic and copies ran while one was open for 1% of the time, Pallas kernels for 0%

commit v1 on v0

v1 whole, which is shorter than its diff:
```python
import functools
import math

import jax
import jax.numpy as jnp
from jax import lax
from jax.experimental import pallas as pl
from jax.experimental.pallas import tpu as pltpu
from jax.sharding import PartitionSpec as P


INV_TEMP = 256
LOG2E = math.log2(math.e)
LANES = 128

NEAR_B = 4

epsilon = 1e-05


HIGH, LOW = 260.0, 52.0
FLOOR = 2.0**-96


def tile(size, most):
    while size % most:
        most //= 2
    return most


def round_up(size, unit):
    return -(-size // unit) * unit


def lanes_of(values, combine):
    total = values[:, :LANES]
    for k in range(1, values.shape[1] // LANES):
        total = combine(total, values[:, k * LANES : (k + 1) * LANES])
    return total


def sublanes_of(values, combine):
    total = values[:8]
    for k in range(1, values.shape[0] // 8):
        total = combine(total, values[k * 8 : (k + 1) * 8])
    return total


def three(value):
    high = value.astype(jnp.bfloat16)
    rest = value - high.astype(jnp.float32)
    middle = rest.astype(jnp.bfloat16)
    low = (rest - middle.astype(jnp.float32)).astype(jnp.bfloat16)
    return [high, middle, low]


def stats_kernel(scale, place_a, place_b, moved, *refs):
    a_parts, refs = refs[: len(place_a)], refs[len(place_a) :]
    b_parts, refs = refs[: len(place_b)], refs[len(place_b) :]
    row_ref, column_ref, a_all, b_all, at, bt, row_one, row_two, column_one, column_two = refs
    tokens, rows = a_all.shape
    columns = b_all.shape[1]
    part_a, part_b = row_ref.shape[1], column_ref.shape[1]
    depth = at.shape[1]
    used = 3 * tokens
    index = [lax.axis_index("aa"), lax.axis_index("ba")] if moved else [0, 0]

    spot = lax.broadcasted_iota(jnp.int32, (rows, depth - used), 1) == 0
    at[:, used:] = jnp.where(spot, -HIGH, 0.0).astype(jnp.bfloat16)
    spot = lax.broadcasted_iota(jnp.int32, (depth - used, columns), 0) == 0
    bt[used:, :] = jnp.where(spot, 1.0, 0.0).astype(jnp.bfloat16)
    for part, places in zip(a_parts, place_a):
        for q, place in enumerate(places):
            first = lax.bitwise_xor(index[1], place) * part_a
            block = part[:, q * part_a : (q + 1) * part_a]
            a_all[:, pl.ds(pl.multiple_of(first, part_a), part_a)] = block
            terms = jnp.concatenate(three(block.astype(jnp.float32) * scale), axis=0)
            for k in range(part_a // LANES):
                here = pl.ds(pl.multiple_of(first + k * LANES, LANES), LANES)
                at[here, :used] = terms[:, k * LANES : (k + 1) * LANES].T
    for part, places in zip(b_parts, place_b):
        for q, place in enumerate(places):
            block = part[:, q * part_b : (q + 1) * part_b]
            here = pl.ds(pl.multiple_of(lax.bitwise_xor(index[0], place) * part_b, part_b), part_b)
            b_all[:, here] = block
            for k in range(3):
                bt[k * tokens : (k + 1) * tokens, here] = block

    wide = tile(columns, 512)
    tall = tile(rows, 512)
    row_one[...] = jnp.zeros_like(row_one)
    row_two[...] = jnp.zeros_like(row_two)

    def over_columns(c, carry):
        here = pl.ds(pl.multiple_of(c * wide, wide), wide)
        one = jnp.zeros((8, wide), jnp.float32)
        two = one
        for k in range(rows // tall):
            band = slice(k * tall, (k + 1) * tall)
            x = jnp.dot(at[band, :], bt[:, here], preferred_element_type=jnp.float32)
            e = jnp.exp2(x)
            row_one[band, :] = row_one[band, :] + lanes_of(e, jnp.add)
            one = one + sublanes_of(e, jnp.add)
            e = jnp.exp2(x + (HIGH - LOW))
            row_two[band, :] = row_two[band, :] + lanes_of(e, jnp.add)
            two = two + sublanes_of(e, jnp.add)
        column_one[:, here] = one
        column_two[:, here] = two
        return carry

    lax.fori_loop(0, columns // wide, over_columns, 0)

    worst = jnp.full((1, LANES), jnp.inf, jnp.float32)

    def pick(one, two):
        return jnp.where(one >= FLOOR, jnp.log2(one) + HIGH, jnp.log2(two) + LOW), jnp.maximum(one, two)

    per_a, per_b = row_ref.shape[1] // LANES, column_ref.shape[1] // LANES
    for k in range(rows // LANES):
        part = slice(k * LANES, (k + 1) * LANES)
        one = jnp.sum(row_one[part, :].T, axis=0, keepdims=True)
        two = jnp.sum(row_two[part, :].T, axis=0, keepdims=True)
        value, least = pick(one, two)
        worst = jnp.minimum(worst, least)
        q, r = k // per_a, k % per_a
        row_ref[q : q + 1, r * LANES : (r + 1) * LANES] = value
    for k in range(columns // LANES):
        part = slice(k * LANES, (k + 1) * LANES)
        one = jnp.sum(column_one[:, part], axis=0, keepdims=True)
        two = jnp.sum(column_two[:, part], axis=0, keepdims=True)
        value, least = pick(one, two)
        worst = jnp.minimum(worst, least)
        q, r = k // per_b, k % per_b
        column_ref[q : q + 1, r * LANES : (r + 1) * LANES] = value

    @pl.when(jnp.min(worst) < FLOOR)
    def exact():
        row_top, row_sum, column_top, column_sum = row_one, row_two, column_one, column_two
        least = jnp.finfo(jnp.float32).min
        row_top[...] = jnp.full_like(row_top, least)
        column_top[...] = jnp.full_like(column_top, least)
        row_sum[...] = jnp.zeros_like(row_sum)
        column_sum[...] = jnp.zeros_like(column_sum)
        low = tile(rows, 128)

        def walk(step):
            def over(k, carry):
                r = pl.ds(pl.multiple_of(lax.rem(k, rows // low) * low, low), low)
                c = pl.ds(pl.multiple_of(lax.div(k, rows // low) * wide, wide), wide)
                step(r, c, jnp.dot(at[r, :], bt[:, c], preferred_element_type=jnp.float32))
                return carry

            lax.fori_loop(0, (rows // low) * (columns // wide), over, 0)

        def tops(r, c, x):
            row_top[r, :] = jnp.maximum(row_top[r, :], lanes_of(x, jnp.maximum))
            column_top[:, c] = jnp.maximum(column_top[:, c], sublanes_of(x, jnp.maximum))

        def sums(r, c, x):
            e = jnp.exp2(x - jnp.concatenate([row_top[r, :]] * (wide // LANES), axis=1))
            row_sum[r, :] = row_sum[r, :] + lanes_of(e, jnp.add)
            e = jnp.exp2(x - jnp.concatenate([column_top[:, c]] * (low // 8), axis=0))
            column_sum[:, c] = column_sum[:, c] + sublanes_of(e, jnp.add)

        walk(tops)
        row_top[...] = jnp.broadcast_to(jnp.max(row_top[...], axis=1, keepdims=True), row_top.shape)
        column_top[...] = jnp.broadcast_to(jnp.max(column_top[...], axis=0, keepdims=True), column_top.shape)
        walk(sums)
        for k in range(rows // LANES):
            part = slice(k * LANES, (k + 1) * LANES)
            mass = jnp.sum(row_sum[part, :].T, axis=0, keepdims=True)
            q, r = k // per_a, k % per_a
            row_ref[q : q + 1, r * LANES : (r + 1) * LANES] = row_top[part, :].T[:1] + (jnp.log2(mass) + HIGH)
        for k in range(columns // LANES):
            part = slice(k * LANES, (k + 1) * LANES)
            mass = jnp.sum(column_sum[:, part], axis=0, keepdims=True)
            q, r = k // per_b, k % per_b
            column_ref[q : q + 1, r * LANES : (r + 1) * LANES] = column_top[:1, part] + (jnp.log2(mass) + HIGH)


def stats(a_parts, b_parts, place_a, place_b, moved, scale):
    tokens = a_parts[0].shape[0]
    rows, columns = (sum(part.shape[1] for part in parts) for parts in (a_parts, b_parts))
    blocks_a, blocks_b = (sum(len(p) for p in place) for place in (place_a, place_b))
    depth = round_up(3 * tokens + 1, LANES)
    vmem = pl.BlockSpec(memory_space=pltpu.VMEM)
    return pl.pallas_call(
        functools.partial(stats_kernel, scale, place_a, place_b, moved),
        out_shape=(
            jax.ShapeDtypeStruct((blocks_a, rows // blocks_a), jnp.float32),
            jax.ShapeDtypeStruct((blocks_b, columns // blocks_b), jnp.float32),
            jax.ShapeDtypeStruct((tokens, rows), jnp.bfloat16),
            jax.ShapeDtypeStruct((tokens, columns), jnp.bfloat16),
        ),
        in_specs=[vmem] * (len(a_parts) + len(b_parts)),
        out_specs=[vmem] * 4,
        scratch_shapes=[
            pltpu.VMEM((rows, depth), jnp.bfloat16),
            pltpu.VMEM((depth, columns), jnp.bfloat16),
            pltpu.VMEM((rows, LANES), jnp.float32),
            pltpu.VMEM((rows, LANES), jnp.float32),
            pltpu.VMEM((8, columns), jnp.float32),
            pltpu.VMEM((8, columns), jnp.float32),
        ],
        cost_estimate=pl.CostEstimate(
            flops=2 * rows * columns * depth, bytes_accessed=0, transcendentals=2 * rows * columns
        ),
        compiler_params=pltpu.CompilerParams(vmem_limit_bytes=32 * 2**20),
        name="stats",
    )(*a_parts, *b_parts)


def joined(parts):
    top = parts[0]
    for part in parts[1:]:
        top = jnp.maximum(top, part)
    mass = jnp.exp2(parts[0] - top)
    for part in parts[1:]:
        mass = mass + jnp.exp2(part - top)
    return top + jnp.log2(mass)


def match_kernel(count_a, count_b, *refs):
    a_ref, b_ref = refs[:2]
    row_parts, refs = refs[2 : 2 + count_a], refs[2 + count_a :]
    column_parts, refs = refs[:count_b], refs[count_b:]
    out_ref, row_level, column_level, at, bt, buffer, done = refs
    tokens, rows = a_ref.shape
    columns = b_ref.shape[1]
    slots, tall, _ = buffer.shape
    depth = at.shape[0]

    def finish(parts, target, level_ref):
        level = joined([part[...] for part in parts]) * (1.0 / (LOG2E * INV_TEMP))
        width = level.shape[1]
        for q in range(level.shape[0]):
            line = level[q : q + 1]
            for k in range(width // LANES):
                spot = q * (width // LANES) + k
                level_ref[spot : spot + 1, :] = line[:, k * LANES : (k + 1) * LANES]
            target(q * width, width, three(line * (-0.5 * tokens)))

    rest = depth - tokens - 6

    def row_terms(first, width, terms):
        one = jnp.ones((3, width), jnp.float32)
        lines = [term.astype(jnp.float32) for term in terms]
        at[tokens:, first : first + width] = jnp.concatenate(
            lines + [one, jnp.zeros((rest, width), jnp.float32)], axis=0
        ).astype(jnp.bfloat16)

    def column_terms(first, width, terms):
        one = jnp.ones((3, width), jnp.float32)
        lines = [term.astype(jnp.float32) for term in terms]
        bt[tokens:, first : first + width] = jnp.concatenate(
            [one] + lines + [jnp.zeros((rest, width), jnp.float32)], axis=0
        ).astype(jnp.bfloat16)

    at[:tokens, :] = a_ref[...]
    bt[:tokens, :] = b_ref[...]
    finish(row_parts, row_terms, row_level)
    finish(column_parts, column_terms, column_level)

    wide = tile(columns, 512)
    tiles = rows // tall

    def copy(t):
        slot = lax.rem(t, slots)
        where = pl.ds(pl.multiple_of(t * tall, tall), tall)
        return pltpu.make_async_copy(buffer.at[slot], out_ref.at[where], done.at[slot])

    def step(t, carry):
        slot = lax.rem(t, slots)

        @pl.when(t >= slots)
        def _():
            copy(t - slots).wait()

        left = at[:, pl.ds(pl.multiple_of(t * tall, tall), tall)].T
        for k in range(columns // wide):
            part = slice(k * wide, (k + 1) * wide)
            dots = jnp.dot(left, bt[:, part], preferred_element_type=jnp.float32)
            buffer[slot, :, part] = dots * (1.0 / tokens)
        copy(t).start()
        return carry

    lax.fori_loop(0, tiles, step, 0)
    for t in range(max(tiles - slots, 0), tiles):
        copy(t).wait()


def match(a, b, row_parts, column_parts):
    tokens, rows = a.shape
    columns = b.shape[1]
    tall = tile(rows, LANES)
    slots = 4
    depth = round_up(tokens + 6, 16)
    vmem = pl.BlockSpec(memory_space=pltpu.VMEM)
    return pl.pallas_call(
        functools.partial(match_kernel, len(row_parts), len(column_parts)),
        out_shape=(
            jax.ShapeDtypeStruct((rows, columns), jnp.float32),
            jax.ShapeDtypeStruct((rows // LANES, LANES), jnp.float32),
            jax.ShapeDtypeStruct((columns // LANES, LANES), jnp.float32),
        ),
        in_specs=[vmem] * (2 + len(row_parts) + len(column_parts)),
        out_specs=(pl.BlockSpec(memory_space=pl.ANY), vmem, vmem),
        scratch_shapes=[
            pltpu.VMEM((depth, rows), jnp.bfloat16),
            pltpu.VMEM((depth, columns), jnp.bfloat16),
            pltpu.VMEM((slots, tall, columns), jnp.float32),
            pltpu.SemaphoreType.DMA((slots,)),
        ],
        cost_estimate=pl.CostEstimate(
            flops=2 * rows * columns * depth, bytes_accessed=4 * rows * columns, transcendentals=0
        ),
        compiler_params=pltpu.CompilerParams(vmem_limit_bytes=32 * 2**20),
        name="match",
    )(a, b, *row_parts, *column_parts)


def slabs_kernel(x_ref, out_ref):
    count, copies, _, depth = out_ref.shape
    for q in range(count):
        part = x_ref[:, q * depth : (q + 1) * depth]
        for c in range(copies):
            out_ref[q, c] = part


def slabs(x, count, copies):
    rows, depth = x.shape[0], x.shape[1] // count
    vmem = pl.BlockSpec(memory_space=pltpu.VMEM)
    return pl.pallas_call(
        slabs_kernel,
        out_shape=jax.ShapeDtypeStruct((count, copies, rows, depth), x.dtype),
        in_specs=[vmem],
        out_specs=vmem,
        compiler_params=pltpu.CompilerParams(vmem_limit_bytes=8 * 2**20),
        name="slabs",
    )(x)


def swap(value, axis, distance):
    size = lax.axis_size(axis)
    return lax.ppermute(value, axis, [(k, k ^ distance) for k in range(size)])


def block_of(value, axis, part, parts, distance):
    size = lax.axis_size(axis)
    width = value.shape[1] // size
    start = (lax.axis_index(axis) ^ distance) * width + part * (width // parts)
    return lax.dynamic_slice_in_dim(value, start, width // parts, axis=1)


def scatter_sum(value, axis, near, parts):
    size = lax.axis_size(axis)
    near = min(near, size)
    far = range(0, size, near)
    width = value.shape[1] // size
    if width % (parts * LANES):
        parts = 1
    first = []
    for part in range(parts):
        sent = [
            jnp.concatenate([block_of(value, axis, part, parts, d ^ k) for k in far], axis=1) for d in range(near)
        ]
        first.append([sent[0]] + [swap(sent[d], axis, d) for d in range(near - 1, 0, -1)])
    done = []
    for got in first:
        total = functools.reduce(jnp.add, got)
        rest = jnp.split(total, len(far), axis=1)
        done.append(functools.reduce(jnp.add, [rest[0]] + [swap(r, axis, k) for r, k in zip(rest[1:], far[1:])]))
    return jnp.concatenate(done, axis=1) if parts > 1 else done[0]


def everyone(value, axis, near):
    size = lax.axis_size(axis)
    near = min(near, size)
    mine = [value] + [swap(value, axis, k) for k in range(near, size, near)]
    mine = jnp.concatenate(mine, axis=1) if len(mine) > 1 else value
    return [mine] + [swap(mine, axis, d) for d in range(near - 1, 0, -1)]


def distances(axis, near):
    near = min(near, lax.axis_size(axis))
    return [0] + list(range(near - 1, 0, -1))


def in_order(parts, axis, near):
    size = lax.axis_size(axis)
    near = min(near, size)
    blocks = [None] * size
    for d, part in zip(distances(axis, near), parts):
        for k, block in enumerate(jnp.split(part, size // near, axis=1)):
            blocks[d ^ (near * k)] = block
    order = lax.axis_index(axis) ^ jnp.arange(size)
    stacked = jnp.take(jnp.stack(blocks), order, axis=0)
    return jnp.transpose(stacked, (1, 0, 2)).reshape(parts[0].shape[0], -1)


def all_joined(value, axis):
    distance = 1
    while distance < lax.axis_size(axis):
        value = joined([value, swap(value, axis, distance)])
        distance *= 2
    return value


def standardize(encoded, bias, axis):
    width = encoded.shape[1]
    bias = lax.dynamic_slice_in_dim(bias, lax.axis_index(axis) * width, width)
    fired = jnp.maximum(encoded + bias[None, :], 0.0)
    centered = fired - jnp.mean(fired, axis=0)[None, :]
    spread = jnp.mean(centered * centered, axis=0)
    return (centered * lax.rsqrt(spread + epsilon)[None, :]).astype(jnp.bfloat16)


def per_device_inner(residual_a, residual_b, encoder_a, bias_a, encoder_b, bias_b):
    size_a, size_b = lax.axis_size("aa"), lax.axis_size("ba")
    index_a = lax.axis_index("aa")
    both = ("aa", "ba")

    own, depth = residual_b.shape[0], residual_b.shape[1] // size_a
    sent = slabs(residual_b, size_a, size_b).reshape(-1, own, depth)
    columns_b = lax.all_to_all(sent, both, 0, 0, tiled=True).reshape(-1, depth)
    partial_b = jnp.dot(columns_b, encoder_b, preferred_element_type=jnp.float32)
    encoded_b = scatter_sum(partial_b, "aa", NEAR_B, 2)

    ratio = size_a // size_b
    assert ratio * size_b == size_a
    tokens_a = lax.all_gather(residual_a, "ba", axis=0, tiled=True)
    tokens = tokens_a.shape[0]
    tokens_a, bias_a, bias_b, _ = lax.optimization_barrier((tokens_a, bias_a, bias_b, partial_b))
    got = []
    for p in range(ratio):
        pairs = [
            ((ratio * j + (i + p) % ratio) * size_b + i // ratio, i * size_b + j)
            for i in range(size_a)
            for j in range(size_b)
        ]
        got.append(lax.ppermute(tokens_a, both, pairs))
    columns_a = [got[0]]
    if ratio > 1:
        turned = jnp.roll(jnp.stack(got), index_a % ratio, axis=0)
        columns_a = [turned[p] for p in range(ratio)]
    columns_a = jnp.concatenate(columns_a, axis=1)
    partial_a = jnp.dot(columns_a, encoder_a, preferred_element_type=jnp.float32)
    encoded_a = scatter_sum(partial_a, "ba", size_b, 1)

    every_a = everyone(standardize(encoded_a, bias_a, "ba"), "ba", size_b)
    every_b = everyone(standardize(encoded_b, bias_b, "aa"), "aa", NEAR_B)

    near = min(NEAR_B, size_a)
    place_a = [[d] for d in distances("ba", size_b)]
    place_b = [[d ^ k for k in range(0, size_a, near)] for d in distances("aa", near)]
    moved = True
    if (bias_a.shape[0] // size_b % LANES or bias_b.shape[0] // size_a % LANES):
        every_a, every_b = [in_order(every_a, "ba", size_b)], [in_order(every_b, "aa", near)]
        place_a, place_b = [[0]], [[0]]
        moved = False
    row_part, column_part, all_a, all_b = stats(every_a, every_b, place_a, place_b, moved, LOG2E * INV_TEMP / tokens)
    column_part = all_joined(column_part, "aa")
    row_part = all_joined(row_part, "ba")
    match_score, row_level, column_level = match(all_a, all_b, [row_part], [column_part])
    return (match_score, row_level.reshape(-1), column_level.reshape(-1))


def solution(mesh):
    return jax.shard_map(
        per_device_inner,
        mesh=mesh,
        in_specs=(
            P("ba", "aa"),
            P(("aa", "ba"), None),
            P("ba", "aa"),
            P("aa"),
            P("aa", "ba"),
            P("ba"),
        ),
        out_specs=(P("aa", "ba"), P("aa"), P("ba")),
        check_vma=False,
    )
```

time: 376 us -> 101 us (0.27)
  blocking collectives: 246 us -> 5.46 us
  other arithmetic: 56.1 us -> 0.64 us
  starting transfers between devices: 0.08 us -> 36.4 us
  Pallas kernels: 0 us -> 24.4 us
  matrix products: 25.9 us -> 3.77 us
  between operations: 15.6 us -> 1.06 us
  waiting for transfers between devices: 31.1 us -> 25.9 us
    psum x6 -> x0, blocking collectives: 119 us -> none  [the longest x1 35 us: per_device(): mean_b = lax.psum(jnp.sum(fired_b, 0), 'aa') / token_total]
    all_gather x4 -> x1, blocking collectives: 74.4 us -> 5.46 us  [per_device_inner(): tokens_a = lax.all_gather(residual_a, 'ba', axis=0, tiled=True)]
    pmax x2 -> x0, blocking collectives: 39.6 us -> none  [the longest x1 33 us: per_device(): column_top = lax.pmax(column_local, 'aa')]
    reduce_sum x5 -> x4, other arithmetic: 30.8 us -> 0.19 us  [the longest x2 0.11 us: standardize(): centered = fired - jnp.mean(fired, axis=0)[None, :]]
    reduce_scatter x1 -> x0, waiting for transfers between devices: 30.5 us -> none  [per_device(): lax.psum_scatter(jnp.dot(inputs, encoder_b, preferred_element_type=jnp.fl...]
    ppermute x0 -> x25, starting transfers between devices: none -> 29.1 us  [the longest x23 27.8 us: swap(): return lax.ppermute(value, axis, [(k, k ^ distance) for k in range(size)])]
    pallas_call x0 -> x3, Pallas kernels: none -> 24.4 us  [the longest x1 12.1 us: match(): pl.pallas_call(functools.partial(match_kernel, len(row_parts), len(column...]
    sub x1 -> x0, other arithmetic: 24.3 us -> none  [per_device(): correlation - 0.5 * (row_level[:, None] + column_level[None, :])]
  transfers between devices with their start and end apart: 2 -> 26, of which waited for: 1 -> 10; matrix products, arithmetic and copies ran while one was open for 1% -> 3% of each run, Pallas kernels for 0% -> 0%
where the time goes in v1:
time: 101 us; the launch traced here: 100 us
  starting transfers between devices  36.4 us (36%)
  waiting for transfers between devices  25.9 us (26%)
  Pallas kernels  24.4 us (24%)
  blocking collectives  5.46 us (5%)
  matrix products  3.77 us (4%)
  local copies, waits for them, and re-layouts  2.46 us (2%)
  between operations  1.06 us (1%)
    ppermute x23, starting transfers between devices, swap(): return lax.ppermute(value, axis, [(k, k ^ distance) for k in range(size)])  27.8 us
    ppermute x23, waiting for transfers between devices, swap(): return lax.ppermute(value, axis, [(k, k ^ distance) for k in range(size)])  24.1 us
    pallas_call x1, Pallas kernels, match(): pl.pallas_call(functools.partial(match_kernel, len(row_parts), len(column...  12.1 us
    pallas_call x1, Pallas kernels, stats(): pl.pallas_call(functools.partial(stats_kernel, scale, place_a, place_b, m...  11.6 us
    all_to_all x1, starting transfers between devices, per_device_inner(): columns_b = lax.all_to_all(sent, both, 0, 0, tiled=True).reshape(-1, depth)  7.33 us
    all_gather x1, blocking collectives, per_device_inner(): tokens_a = lax.all_gather(residual_a, 'ba', axis=0, tiled=True)  5.46 us
    dot_general x1, matrix products, per_device_inner(): jnp.dot(columns_b, encoder_b, preferred_element_type=jnp.float32)  2.93 us
  transfers between devices with their start and end apart: 26, of which 10 were waited for; matrix products, arithmetic and copies ran while one was open for 3% of the time, Pallas kernels for 0%

profile of v1, /device:TPU:0, one launch (start us, length us, event | category | flops | bytes accessed | tf_op | source)
XLA Modules:
  0.0 100.2 jit_solution(18172747971223750783)
XLA Ops:
  2.0 7.3 %all-to-all-start = ((bf16[32,2,448]{2,1,0:T(2,128)(2,1)}), bf16[32,2,448]{2,1,0:T(2,128)(2,1)S(1)}, u32[]{:S(2)}, u32[]{:S(2)}) async-start(bf16[32,2,448]{2,1,0:T(2,128)(2,1)} %bitcast), calls=%async_computation | async-start | bytes 131072 | tf_op jit(solution)/shard_map/all_to_all | solution.py:425
  9.5 5.5 %all_gather.3 = bf16[64,512]{1,0:T(8,128)(2,1)S(1)} all-gather(bf16[16,512]{1,0:T(8,128)(2,1)} %param.6), channel_id=1, replica_groups=mesh['aa'=8,'ba'=4] {'ba'}, dimensions={0}, use_global_device_ids=true | all-gather | bytes 81920 | tf_op jit(solution)/shard_map/all_gather | solution.py:431
  15.0 1.8 %all-to-all-done = bf16[32,2,448]{2,1,0:T(2,128)(2,1)S(1)} async-done(((bf16[32,2,448]{2,1,0:T(2,128)(2,1)}), bf16[32,2,448]{2,1,0:T(2,128)(2,1)S(1)}, u32[]{:S(2)}, u32[]{:S(2)}) %all-to-all-start) | async-done | bytes 57376 | tf_op jit(solution)/shard_map/all_to_all | solution.py:425
  16.9 2.9 %fusion.25 = f32[64,4096]{1,0:T(8,128)S(1)} fusion(bf16[64,448]{1,0:T(8,128)(2,1)S(1)} %reshape.37, bf16[448,4096]{1,0:T(8,128)(2,1)} %param.10), kind=kOutput, calls=%fused_computation.81 | convolution fusion | flops 234881024 | bytes 4775936 | tf_op jit(solution)/shard_map/dot_general | solution.py:426
  22.0 4.0 %collective-permute-start.8 = (f32[64,512]{1,0:T(8,128)S(1)}, f32[64,512]{1,0:T(8,128)S(1)}, u32[]{:S(2)}, u32[]{:S(2)}) collective-permute-start(f32[64,512]{1,0:T(8,128)S(1)} %pad_maximum_fusion), channel_id=1, source_target_pairs={{0,12},{4,8},{8,4},{12,0},{16,28},{20,24},{24,20},{28,16},{1,13},{... | collective-permute-start | bytes 393224 | tf_op jit(solution)/shard_map/ppermute | solution.py:345
  27.8 2.7 %collective-permute-start.12 = (f32[64,512]{1,0:T(8,128)S(1)}, f32[64,512]{1,0:T(8,128)S(1)}, u32[]{:S(2)}, u32[]{:S(2)}) collective-permute-start(f32[64,512]{1,0:T(8,128)S(1)} %pad_maximum_fusion.3), channel_id=1, source_target_pairs={{0,12},{4,8},{8,4},{12,0},{16,28},{20,24},{24,20},{28,16},{1,13},{... | collective-permute-start | bytes 393224 | tf_op jit(solution)/shard_map/ppermute | solution.py:345
  32.5 1.6 %collective-permute-done.9 = f32[64,512]{1,0:T(8,128)S(1)} collective-permute-done((f32[64,512]{1,0:T(8,128)S(1)}, f32[64,512]{1,0:T(8,128)S(1)}, u32[]{:S(2)}, u32[]{:S(2)}) %collective-permute-start.9) | collective-permute-done | bytes 131104 | tf_op jit(solution)/shard_map/ppermute | solution.py:345
  34.0 2.3 %collective-permute-start.2 = (f32[64,512]{1,0:T(8,128)S(1)}, f32[64,512]{1,0:T(8,128)S(1)}, u32[]{:S(2)}, u32[]{:S(2)}) collective-permute-start(f32[64,512]{1,0:T(8,128)S(1)} %get-tuple-element.41), channel_id=1, source_target_pairs={{0,3},{1,2},{2,1},{3,0},{4,7},{5,6},{6,5},{7,4},{8,11},{9,10},{10,... | collective-permute-start | bytes 393224 | tf_op jit(solution)/shard_map/ppermute | solution.py:345
  37.3 3.2 %collective-permute-start.3 = (f32[64,512]{1,0:T(8,128)S(1)}, f32[64,512]{1,0:T(8,128)S(1)}, u32[]{:S(2)}, u32[]{:S(2)}) collective-permute-start(f32[64,512]{1,0:T(8,128)S(1)} %get-tuple-element.43), channel_id=1, source_target_pairs={{0,2},{1,3},{2,0},{3,1},{4,6},{5,7},{6,4},{7,5},{8,10},{9,11},{10,... | collective-permute-start | bytes 393224 | tf_op jit(solution)/shard_map/ppermute | solution.py:345
  40.4 2.0 %collective-permute-start.11 = (f32[64,256]{1,0:T(8,128)S(1)}, f32[64,256]{1,0:T(8,128)S(1)}, u32[]{:S(2)}, u32[]{:S(2)}) collective-permute-start(f32[64,256]{1,0:T(8,128)S(1)} %split.17), channel_id=1, source_target_pairs={{0,16},{4,20},{8,24},{12,28},{16,0},{20,4},{24,8},{28,12},{1,17},{... | collective-permute-start | bytes 196616 | tf_op jit(solution)/shard_map/ppermute | solution.py:345
  43.5 4.0 %collective-permute-done.11 = f32[64,256]{1,0:T(8,128)S(1)} collective-permute-done((f32[64,256]{1,0:T(8,128)S(1)}, f32[64,256]{1,0:T(8,128)S(1)}, u32[]{:S(2)}, u32[]{:S(2)}) %collective-permute-start.11) | collective-permute-done | bytes 65568 | tf_op jit(solution)/shard_map/ppermute | solution.py:345
  47.5 1.5 %collective-permute-done.15 = f32[64,256]{1,0:T(8,128)S(1)} collective-permute-done((f32[64,256]{1,0:T(8,128)S(1)}, f32[64,256]{1,0:T(8,128)S(1)}, u32[]{:S(2)}, u32[]{:S(2)}) %collective-permute-start.15) | collective-permute-done | bytes 65568 | tf_op jit(solution)/shard_map/ppermute | solution.py:345
  49.5 4.9 %collective-permute-done.16 = bf16[64,512]{1,0:T(8,128)(2,1)S(1)} collective-permute-done((bf16[64,512]{1,0:T(8,128)(2,1)S(1)}, bf16[64,512]{1,0:T(8,128)(2,1)S(1)}, u32[]{:S(2)}, u32[]{:S(2)}) %collective-permute-start.16) | collective-permute-done | bytes 65568 | tf_op jit(solution)/shard_map/ppermute | solution.py:345
  54.4 1.5 %collective-permute-start.19 = (bf16[64,1024]{1,0:T(8,128)(2,1)S(1)}, bf16[64,1024]{1,0:T(8,128)(2,1)S(1)}, u32[]{:S(2)}, u32[]{:S(2)}) collective-permute-start(bf16[64,1024]{1,0:T(8,128)(2,1)S(1)} %pad_maximum_fusion.6.refs_4_), channel_id=1, source_target_pairs={{0,4},{4,0},{8,12},{12,8},{16,20},{20,16},{24,28},{28,24},{1,5},{5... | collective-permute-start | bytes 393224 | tf_op jit(solution)/shard_map/ppermute | solution.py:345
  55.9 2.1 %collective-permute-start.17 = (bf16[64,1024]{1,0:T(8,128)(2,1)S(1)}, bf16[64,1024]{1,0:T(8,128)(2,1)S(1)}, u32[]{:S(2)}, u32[]{:S(2)}) collective-permute-start(bf16[64,1024]{1,0:T(8,128)(2,1)S(1)} %pad_maximum_fusion.6.refs_4_), channel_id=1, source_target_pairs={{0,12},{4,8},{8,4},{12,0},{16,28},{20,24},{24,20},{28,16},{1,13},{... | collective-permute-start | bytes 393224 | tf_op jit(solution)/shard_map/ppermute | solution.py:345
  58.0 2.4 %collective-permute-start.6 = (bf16[64,512]{1,0:T(8,128)(2,1)S(1)}, bf16[64,512]{1,0:T(8,128)(2,1)S(1)}, u32[]{:S(2)}, u32[]{:S(2)}) collective-permute-start(bf16[64,512]{1,0:T(8,128)(2,1)S(1)} %multiply_convert_fusion.1.refs_0_), channel_id=1, source_target_pairs={{0,2},{1,3},{2,0},{3,1},{4,6},{5,7},{6,4},{7,5},{8,10},{9,11},{10,... | collective-permute-start | bytes 196616 | tf_op jit(solution)/shard_map/ppermute | solution.py:345
  60.3 2.2 %collective-permute-done.6.refs_2_ = bf16[64,512]{1,0:T(8,128)(2,1)S(1)} collective-permute-done((bf16[64,512]{1,0:T(8,128)(2,1)S(1)}, bf16[64,512]{1,0:T(8,128)(2,1)S(1)}, u32[]{:S(2)}, u32[]{:S(2)}) %collective-permute-start.6) | collective-permute-done | bytes 65568 | tf_op jit(solution)/shard_map/ppermute | solution.py:345
  62.6 1.5 %collective-permute-done.5.refs_1_ = bf16[64,512]{1,0:T(8,128)(2,1)S(1)} collective-permute-done((bf16[64,512]{1,0:T(8,128)(2,1)S(1)}, bf16[64,512]{1,0:T(8,128)(2,1)S(1)}, u32[]{:S(2)}, u32[]{:S(2)}) %collective-permute-start.5) | collective-permute-done | bytes 65568 | tf_op jit(solution)/shard_map/ppermute | solution.py:345
  64.0 11.6 %stats.1 = (f32[4,512]{1,0:T(4,128)S(1)}, f32[8,512]{1,0:T(8,128)S(1)}, bf16[64,2048]{1,0:T(8,128)(2,1)S(1)}, bf16[64,4096]{1,0:T(8,128)(2,1)S(1)}) custom-call(bf16[64,512]{1,0:T(8,128)(2,1)S(1)} %multiply_convert_fusion.1.refs_0_, bf16[64,512]{1,0:T(8,128)(2,1)S(1)} %collective-permute-done.5.refs_1_, bf16[64,512]{1,0:T(8,128)(2,1)S(1)} %collective-permute-done.6.refs_2_, ...), custom_call_target="tpu_custom_call" | custom-call | flops 4294967296 | tf_op jit(solution)/shard_map/stats/pallas_call | solution.py:187
  77.0 2.5 %collective-permute-done.22 = f32[8,512]{1,0:T(8,128)S(1)} collective-permute-done((f32[8,512]{1,0:T(8,128)S(1)}, f32[8,512]{1,0:T(8,128)S(1)}, u32[]{:S(2)}, u32[]{:S(2)}) %collective-permute-start.22) | collective-permute-done | bytes 16416 | tf_op jit(solution)/shard_map/ppermute | solution.py:345
  79.6 2.1 %collective-permute-start.21 = (f32[4,512]{1,0:T(4,128)S(1)}, f32[4,512]{1,0:T(4,128)S(1)}, u32[]{:S(2)}, u32[]{:S(2)}) collective-permute-start(f32[4,512]{1,0:T(4,128)S(1)} %multiply_add_fusion.4), channel_id=1, source_target_pairs={{0,2},{1,3},{2,0},{3,1},{4,6},{5,7},{6,4},{7,5},{8,10},{9,11},{10,... | collective-permute-start | bytes 24584 | tf_op jit(solution)/shard_map/ppermute | solution.py:345
  81.7 1.6 %collective-permute-done.23 = f32[8,512]{1,0:T(8,128)S(1)} collective-permute-done((f32[8,512]{1,0:T(8,128)S(1)}, f32[8,512]{1,0:T(8,128)S(1)}, u32[]{:S(2)}, u32[]{:S(2)}) %collective-permute-start.23) | collective-permute-done | bytes 16416 | tf_op jit(solution)/shard_map/ppermute | solution.py:345
  83.7 4.3 %collective-permute-done.24 = f32[8,512]{1,0:T(8,128)S(1)} collective-permute-done((f32[8,512]{1,0:T(8,128)S(1)}, f32[8,512]{1,0:T(8,128)S(1)}, u32[]{:S(2)}, u32[]{:S(2)}) %collective-permute-start.24) | collective-permute-done | bytes 16416 | tf_op jit(solution)/shard_map/ppermute | solution.py:345
  88.0 12.1 %match.1 = (f32[2048,4096]{1,0:T(8,128)}, f32[16,128]{1,0:T(8,128)}, f32[32,128]{1,0:T(8,128)}) custom-call(bf16[64,2048]{1,0:T(8,128)(2,1)S(1)} %get-tuple-element.16.refs_0_, bf16[64,4096]{1,0:T(8,128)(2,1)S(1)} %get-tuple-element.17.refs_1_, f32[4,512]{1,0:T(4,128)S(1)} %multiply_add_fusion.3.refs_2_, f32[8,512]{1,0:T(8,128)S(1)} %multiply_add_fusion.refs_3_), custom_call_target="tpu_custom_call" | custom-call | flops 1342177280 | bytes 33554432 | tf_op jit(solution)/shard_map/match/pallas_call | solution.py:299
  (73 shorter events, 11.7 us)
Async XLA Ops:
  2.0 14.7 %all-to-all-start = ((bf16[32,2,448]{2,1,0:T(2,128)(2,1)}), bf16[32,2,448]{2,1,0:T(2,128)(2,1)S(1)}, u32[]{:S(2)}, u32[]{:S(2)}) async-start(bf16[32,2,448]{2,1,0:T(2,128)(2,1)} %bitcast), calls=%async_computation | async-start | bytes 131072 | tf_op jit(solution)/shard_map/all_to_all | solution.py:425
  19.8 8.0 %collective-permute-start.1 = (bf16[64,512]{1,0:T(8,128)(2,1)S(1)}, bf16[64,512]{1,0:T(8,128)(2,1)S(1)}, u32[]{:S(2)}, u32[]{:S(2)}) collective-permute-start(bf16[64,512]{1,0:T(8,128)(2,1)S(1)} %all_gather.3), channel_id=1, source_target_pairs={{4,0},{12,1},{20,2},{28,3},{0,4},{8,5},{16,6},{24,7},{5,8},{13,9},... | collective-permute-start | bytes 196616 | tf_op jit(solution)/shard_map/ppermute | solution.py:441
  20.5 10.0 %collective-permute-start = (bf16[64,512]{1,0:T(8,128)(2,1)S(1)}, bf16[64,512]{1,0:T(8,128)(2,1)S(1)}, u32[]{:S(2)}, u32[]{:S(2)}) collective-permute-start(bf16[64,512]{1,0:T(8,128)(2,1)S(1)} %all_gather.3), channel_id=1, source_target_pairs={{0,0},{8,1},{16,2},{24,3},{4,4},{12,5},{20,6},{28,7},{1,8},{9,9},{... | collective-permute-start | bytes 196616 | tf_op jit(solution)/shard_map/ppermute | solution.py:441
  22.0 9.5 %collective-permute-start.8 = (f32[64,512]{1,0:T(8,128)S(1)}, f32[64,512]{1,0:T(8,128)S(1)}, u32[]{:S(2)}, u32[]{:S(2)}) collective-permute-start(f32[64,512]{1,0:T(8,128)S(1)} %pad_maximum_fusion), channel_id=1, source_target_pairs={{0,12},{4,8},{8,4},{12,0},{16,28},{20,24},{24,20},{28,16},{1,13},{... | collective-permute-start | bytes 393224 | tf_op jit(solution)/shard_map/ppermute | solution.py:345
  26.0 8.0 %collective-permute-start.9 = (f32[64,512]{1,0:T(8,128)S(1)}, f32[64,512]{1,0:T(8,128)S(1)}, u32[]{:S(2)}, u32[]{:S(2)}) collective-permute-start(f32[64,512]{1,0:T(8,128)S(1)} %pad_maximum_fusion.1), channel_id=1, source_target_pairs={{0,8},{4,12},{8,0},{12,4},{16,24},{20,28},{24,16},{28,20},{1,9},{5... | collective-permute-start | bytes 393224 | tf_op jit(solution)/shard_map/ppermute | solution.py:345
  26.1 10.2 %collective-permute-start.10 = (f32[64,512]{1,0:T(8,128)S(1)}, f32[64,512]{1,0:T(8,128)S(1)}, u32[]{:S(2)}, u32[]{:S(2)}) collective-permute-start(f32[64,512]{1,0:T(8,128)S(1)} %pad_maximum_fusion.2), channel_id=1, source_target_pairs={{0,4},{4,0},{8,12},{12,8},{16,20},{20,16},{24,28},{28,24},{1,5},{5... | collective-permute-start | bytes 393224 | tf_op jit(solution)/shard_map/ppermute | solution.py:345
  27.8 9.5 %collective-permute-start.12 = (f32[64,512]{1,0:T(8,128)S(1)}, f32[64,512]{1,0:T(8,128)S(1)}, u32[]{:S(2)}, u32[]{:S(2)}) collective-permute-start(f32[64,512]{1,0:T(8,128)S(1)} %pad_maximum_fusion.3), channel_id=1, source_target_pairs={{0,12},{4,8},{8,4},{12,0},{16,28},{20,24},{24,20},{28,16},{1,13},{... | collective-permute-start | bytes 393224 | tf_op jit(solution)/shard_map/ppermute | solution.py:345
  30.5 9.9 %collective-permute-start.13 = (f32[64,512]{1,0:T(8,128)S(1)}, f32[64,512]{1,0:T(8,128)S(1)}, u32[]{:S(2)}, u32[]{:S(2)}) collective-permute-start(f32[64,512]{1,0:T(8,128)S(1)} %pad_maximum_fusion.4), channel_id=1, source_target_pairs={{0,8},{4,12},{8,0},{12,4},{16,24},{20,28},{24,16},{28,20},{1,9},{5... | collective-permute-start | bytes 393224 | tf_op jit(solution)/shard_map/ppermute | solution.py:345
  31.6 10.8 %collective-permute-start.14 = (f32[64,512]{1,0:T(8,128)S(1)}, f32[64,512]{1,0:T(8,128)S(1)}, u32[]{:S(2)}, u32[]{:S(2)}) collective-permute-start(f32[64,512]{1,0:T(8,128)S(1)} %pad_maximum_fusion.5), channel_id=1, source_target_pairs={{0,4},{4,0},{8,12},{12,8},{16,20},{20,16},{24,28},{28,24},{1,5},{5... | collective-permute-start | bytes 393224 | tf_op jit(solution)/shard_map/ppermute | solution.py:345
  34.0 15.2 %collective-permute-start.2 = (f32[64,512]{1,0:T(8,128)S(1)}, f32[64,512]{1,0:T(8,128)S(1)}, u32[]{:S(2)}, u32[]{:S(2)}) collective-permute-start(f32[64,512]{1,0:T(8,128)S(1)} %get-tuple-element.41), channel_id=1, source_target_pairs={{0,3},{1,2},{2,1},{3,0},{4,7},{5,6},{6,5},{7,4},{8,11},{9,10},{10,... | collective-permute-start | bytes 393224 | tf_op jit(solution)/shard_map/ppermute | solution.py:345
  36.3 12.9 %collective-permute-start.4 = (f32[64,512]{1,0:T(8,128)S(1)}, f32[64,512]{1,0:T(8,128)S(1)}, u32[]{:S(2)}, u32[]{:S(2)}) collective-permute-start(f32[64,512]{1,0:T(8,128)S(1)} %get-tuple-element.42), channel_id=1, source_target_pairs={{0,1},{1,0},{2,3},{3,2},{4,5},{5,4},{6,7},{7,6},{8,9},{9,8},{10,11... | collective-permute-start | bytes 393224 | tf_op jit(solution)/shard_map/ppermute | solution.py:345
  37.3 12.0 %collective-permute-start.3 = (f32[64,512]{1,0:T(8,128)S(1)}, f32[64,512]{1,0:T(8,128)S(1)}, u32[]{:S(2)}, u32[]{:S(2)}) collective-permute-start(f32[64,512]{1,0:T(8,128)S(1)} %get-tuple-element.43), channel_id=1, source_target_pairs={{0,2},{1,3},{2,0},{3,1},{4,6},{5,7},{6,4},{7,5},{8,10},{9,11},{10,... | collective-permute-start | bytes 393224 | tf_op jit(solution)/shard_map/ppermute | solution.py:345
  40.4 7.1 %collective-permute-start.11 = (f32[64,256]{1,0:T(8,128)S(1)}, f32[64,256]{1,0:T(8,128)S(1)}, u32[]{:S(2)}, u32[]{:S(2)}) collective-permute-start(f32[64,256]{1,0:T(8,128)S(1)} %split.17), channel_id=1, source_target_pairs={{0,16},{4,20},{8,24},{12,28},{16,0},{20,4},{24,8},{28,12},{1,17},{... | collective-permute-start | bytes 196616 | tf_op jit(solution)/shard_map/ppermute | solution.py:345
  42.5 6.6 %collective-permute-start.15 = (f32[64,256]{1,0:T(8,128)S(1)}, f32[64,256]{1,0:T(8,128)S(1)}, u32[]{:S(2)}, u32[]{:S(2)}) collective-permute-start(f32[64,256]{1,0:T(8,128)S(1)} %split.19), channel_id=1, source_target_pairs={{0,16},{4,20},{8,24},{12,28},{16,0},{20,4},{24,8},{28,12},{1,17},{... | collective-permute-start | bytes 196616 | tf_op jit(solution)/shard_map/ppermute | solution.py:345
  49.2 5.2 %collective-permute-start.16 = (bf16[64,512]{1,0:T(8,128)(2,1)S(1)}, bf16[64,512]{1,0:T(8,128)(2,1)S(1)}, u32[]{:S(2)}, u32[]{:S(2)}) collective-permute-start(bf16[64,512]{1,0:T(8,128)(2,1)S(1)} %multiply_convert_fusion), channel_id=1, source_target_pairs={{0,16},{4,20},{8,24},{12,28},{16,0},{20,4},{24,8},{28,12},{1,17},{... | collective-permute-start | bytes 196616 | tf_op jit(solution)/shard_map/ppermute | solution.py:345
  49.4 10.9 %collective-permute-start.7 = (bf16[64,512]{1,0:T(8,128)(2,1)S(1)}, bf16[64,512]{1,0:T(8,128)(2,1)S(1)}, u32[]{:S(2)}, u32[]{:S(2)}) collective-permute-start(bf16[64,512]{1,0:T(8,128)(2,1)S(1)} %multiply_convert_fusion.1.refs_0_), channel_id=1, source_target_pairs={{0,1},{1,0},{2,3},{3,2},{4,5},{5,4},{6,7},{7,6},{8,9},{9,8},{10,11... | collective-permute-start | bytes 196616 | tf_op jit(solution)/shard_map/ppermute | solution.py:345
  54.4 9.6 %collective-permute-start.19 = (bf16[64,1024]{1,0:T(8,128)(2,1)S(1)}, bf16[64,1024]{1,0:T(8,128)(2,1)S(1)}, u32[]{:S(2)}, u32[]{:S(2)}) collective-permute-start(bf16[64,1024]{1,0:T(8,128)(2,1)S(1)} %pad_maximum_fusion.6.refs_4_), channel_id=1, source_target_pairs={{0,4},{4,0},{8,12},{12,8},{16,20},{20,16},{24,28},{28,24},{1,5},{5... | collective-permute-start | bytes 393224 | tf_op jit(solution)/shard_map/ppermute | solution.py:345
  55.9 8.1 %collective-permute-start.18 = (bf16[64,1024]{1,0:T(8,128)(2,1)S(1)}, bf16[64,1024]{1,0:T(8,128)(2,1)S(1)}, u32[]{:S(2)}, u32[]{:S(2)}) collective-permute-start(bf16[64,1024]{1,0:T(8,128)(2,1)S(1)} %pad_maximum_fusion.6.refs_4_), channel_id=1, source_target_pairs={{0,8},{4,12},{8,0},{12,4},{16,24},{20,28},{24,16},{28,20},{1,9},{5... | collective-permute-start | bytes 393224 | tf_op jit(solution)/shard_map/ppermute | solution.py:345
  55.9 8.1 %collective-permute-start.17 = (bf16[64,1024]{1,0:T(8,128)(2,1)S(1)}, bf16[64,1024]{1,0:T(8,128)(2,1)S(1)}, u32[]{:S(2)}, u32[]{:S(2)}) collective-permute-start(bf16[64,1024]{1,0:T(8,128)(2,1)S(1)} %pad_maximum_fusion.6.refs_4_), channel_id=1, source_target_pairs={{0,12},{4,8},{8,4},{12,0},{16,28},{20,24},{24,20},{28,16},{1,13},{... | collective-permute-start | bytes 393224 | tf_op jit(solution)/shard_map/ppermute | solution.py:345
  58.0 4.6 %collective-permute-start.6 = (bf16[64,512]{1,0:T(8,128)(2,1)S(1)}, bf16[64,512]{1,0:T(8,128)(2,1)S(1)}, u32[]{:S(2)}, u32[]{:S(2)}) collective-permute-start(bf16[64,512]{1,0:T(8,128)(2,1)S(1)} %multiply_convert_fusion.1.refs_0_), channel_id=1, source_target_pairs={{0,2},{1,3},{2,0},{3,1},{4,6},{5,7},{6,4},{7,5},{8,10},{9,11},{10,... | collective-permute-start | bytes 196616 | tf_op jit(solution)/shard_map/ppermute | solution.py:345
  75.6 3.8 %collective-permute-start.22 = (f32[8,512]{1,0:T(8,128)S(1)}, f32[8,512]{1,0:T(8,128)S(1)}, u32[]{:S(2)}, u32[]{:S(2)}) collective-permute-start(f32[8,512]{1,0:T(8,128)S(1)} %get-tuple-element.19), channel_id=1, source_target_pairs={{0,4},{4,0},{8,12},{12,8},{16,20},{20,16},{24,28},{28,24},{1,5},{5... | collective-permute-start | bytes 49160 | tf_op jit(solution)/shard_map/ppermute | solution.py:345
  79.5 3.8 %collective-permute-start.23 = (f32[8,512]{1,0:T(8,128)S(1)}, f32[8,512]{1,0:T(8,128)S(1)}, u32[]{:S(2)}, u32[]{:S(2)}) collective-permute-start(f32[8,512]{1,0:T(8,128)S(1)} %multiply_add_fusion.2), channel_id=1, source_target_pairs={{0,8},{4,12},{8,0},{12,4},{16,24},{20,28},{24,16},{28,20},{1,9},{5... | collective-permute-start | bytes 49160 | tf_op jit(solution)/shard_map/ppermute | solution.py:345
  79.6 4.0 %collective-permute-start.21 = (f32[4,512]{1,0:T(4,128)S(1)}, f32[4,512]{1,0:T(4,128)S(1)}, u32[]{:S(2)}, u32[]{:S(2)}) collective-permute-start(f32[4,512]{1,0:T(4,128)S(1)} %multiply_add_fusion.4), channel_id=1, source_target_pairs={{0,2},{1,3},{2,0},{3,1},{4,6},{5,7},{6,4},{7,5},{8,10},{9,11},{10,... | collective-permute-start | bytes 24584 | tf_op jit(solution)/shard_map/ppermute | solution.py:345
  83.3 4.7 %collective-permute-start.24 = (f32[8,512]{1,0:T(8,128)S(1)}, f32[8,512]{1,0:T(8,128)S(1)}, u32[]{:S(2)}, u32[]{:S(2)}) collective-permute-start(f32[8,512]{1,0:T(8,128)S(1)} %multiply_add_fusion.1), channel_id=1, source_target_pairs={{0,16},{4,20},{8,24},{12,28},{16,0},{20,4},{24,8},{28,12},{1,17},{... | collective-permute-start | bytes 49160 | tf_op jit(solution)/shard_map/ppermute | solution.py:345
  (4 other events, 20.8 us)
